TPU v7x, 256 devices: a 8x8x2 block of a 8x8x16 slice. The times are simulated.
256 devices in a mesh: groups: 2 (over z), seq: 16 (over x, core), qset: 8 (over y).
Axes of the slice: x: 8, y: 8, z: 2, core: 2. Of those that a mesh axis runs over, the one named last changes fastest.
The devices are a block of a 8x8x16 slice.
Arguments:
- states: bfloat16 [16, 16, 128, 4096], P(('groups', 'qset'), 'seq'), parts along dimension 0, may hold values from -7 to 7
- enc_gain: bfloat16 [4096], replicated, may hold values from 0.25 to 1.75
- dec_states: bfloat16 [32, 64, 4096], P(('groups', 'qset')), parts along dimension 0, may hold values from -7 to 7
- dec_gain: bfloat16 [4096], replicated, may hold values from 0.25 to 1.75
- query_weight: bfloat16 [4096, 4096], P(None, 'seq'), may hold values from -0.375 to 0.375
- key_value_weight: bfloat16 [4096, 2, 4096], P(None, None, 'seq'), may hold values from -0.0625 to 0.0625
- out_weight: bfloat16 [4096, 4096], P('seq'), may hold values from -0.75 to 0.75
- question_of: int32 [16, 16, 1], P('groups'), parts along dimension 0, may hold values from 0 to 15; in each aligned block of 16 rows (0 to 15, 16 to 31, ..., all dimensions but the last counted through in order) at most 2 rows name the same one
Outputs:
- mixed: bfloat16 [32, 64, 4096], P(('groups', 'qset'), None, 'seq'), parts along dimension 0
There are 2 independent parts, one for each index of `groups`. A program takes and returns all parts, laid end to end along the dimension named above; an argument that names none is the same for every part. Nothing has to cross between parts.
Inputs may be any that keep to these rules, and one draw needn't show every extreme that they name: `question_of`: within each index of the first dimension (one source group of 16 passages) at most 2 passages name the same question, and exactly 2 do for some question in some groups; every question is named by at least one passage.
All inputs are finite; a program needn't handle non-finite values.
Results may differ from a plain program's by a relative error of at most 0.014.
The roundings to bfloat16 on the way count: a program that leaves them out, or rounds other values in their place, can miss the bound.
Values may be sent and summed in bfloat16 or wider, within the bound.
A program may use at most 128 MiB of HBM per device.

v0:
```python
import math
import jax
import jax.numpy as jnp
from jax import lax
from jax.sharding import PartitionSpec as P

HD = 64
CAP = 2
EPSILON = 1e-06
MASKED_SCORE = -1e30


def from_everyone(shard, axis):
    devices = lax.axis_size(axis)
    return lax.all_to_all(
        jnp.broadcast_to(shard[None], (devices, *shard.shape)), axis, 0, 0, tiled=True
    )


def laid_out(pieces, dim):
    dims = list(pieces.shape[1:])
    dims[dim] *= pieces.shape[0]
    return jnp.moveaxis(pieces, 0, dim).reshape(dims)


def gather_directly(shard, axis, dim):
    pieces = from_everyone(shard, axis)
    return laid_out(pieces, dim)


def over_copies(shard, axis):
    return from_everyone(shard, axis).max(axis=0)


def split_up(shard, dim, devices):
    dims = shard.shape
    pieces = shard.reshape(*dims[:dim], devices, dims[dim] // devices, *dims[dim + 1 :])
    return jnp.moveaxis(pieces, dim, 0)


def sent_and_summed(shard, axis, dim):
    pieces = split_up(shard, dim, lax.axis_size(axis))
    arrived = lax.all_to_all(pieces, axis, split_axis=0, concat_axis=0, tiled=True)
    return arrived.astype(jnp.float32).sum(axis=0)


def sent_together(arrays, axis, dim, along):
    widths = [math.prod(a.shape[along:]) for a in arrays]
    both = jnp.concatenate(
        [a.reshape(*a.shape[:along], w) for a, w in zip(arrays, widths)], axis=along
    )
    result = sent_and_summed(both, axis, dim)
    pieces = jnp.split(result, [sum(widths[:k]) for k in range(1, len(widths))], axis=along)
    return tuple(
        (b.reshape(*result.shape[:along], *a.shape[along:]) for a, b in zip(arrays, pieces))
    )


def scaled_norm(rows_in, gain_vec):
    rows_f32 = rows_in.astype(jnp.float32)
    mean_square = jnp.mean(rows_f32 * rows_f32, axis=-1, keepdims=True)
    return rows_f32 * lax.rsqrt(mean_square + EPSILON) * gain_vec.astype(jnp.float32)


def body(
    states, enc_gain, dec_states, dec_gain, query_weight, key_value_weight, out_weight, question_of
):
    model_width = states.shape[-1]
    passage_len = states.shape[2]
    group_count = lax.axis_size("qset")
    shard_count = lax.axis_size("seq")
    group_index = lax.axis_index("qset")
    shard_index = lax.axis_index("seq")
    local_questions = dec_states.shape[0]
    dec_len = dec_states.shape[1]
    head_cols = query_weight.shape[1]
    heads_here = head_cols // HD
    all_questions = local_questions * group_count
    kv_weight = key_value_weight.reshape(model_width, 2 * head_cols)
    own_rows = scaled_norm(states[0, 0], enc_gain).astype(jnp.bfloat16)[None]
    gathered_rows = lax.all_gather(own_rows, "seq", axis=0, tiled=True)
    piece_count = gathered_rows.shape[0]
    flat_rows = gathered_rows.reshape(piece_count * passage_len, model_width)
    product = jnp.dot(flat_rows, kv_weight, preferred_element_type=jnp.float32)
    key_vals = product.astype(jnp.bfloat16).reshape(piece_count, passage_len, 2 * head_cols)
    passage_table = question_of[:, :, 0]
    numbers = jnp.arange(all_questions, dtype=jnp.int32)
    counts = jnp.sum(
        (passage_table[:, :, None] == numbers[None, None, :]).astype(jnp.int32), axis=1
    )
    group_table = lax.dynamic_index_in_dim(passage_table, group_index, 0, keepdims=False)
    matches = (group_table[:, None] == numbers[None, :]).astype(jnp.int32)
    earlier = jnp.cumsum(matches, axis=0) - matches
    slot_rank = jnp.sum(earlier * matches, axis=1)
    slot_index = group_table * CAP + slot_rank
    picker = (
        jnp.arange(all_questions * CAP, dtype=jnp.int32)[:, None] == slot_index[None, :]
    ).astype(jnp.bfloat16)
    packed = jnp.einsum("as,spc->apc", picker, key_vals, preferred_element_type=jnp.float32).astype(
        jnp.bfloat16
    )
    dec_rows = (
        scaled_norm(dec_states, dec_gain)
        .astype(jnp.bfloat16)
        .reshape(local_questions * dec_len, model_width)
    )
    queries = jnp.dot(dec_rows, query_weight, preferred_element_type=jnp.float32)
    queries = queries.astype(jnp.bfloat16).reshape(local_questions, dec_len, heads_here, HD)
    slot_numbers = jnp.arange(CAP, dtype=jnp.int32)
    gathered = gather_directly(queries, "qset", 0)
    local_keys = packed.reshape(all_questions, CAP * passage_len, 2 * head_cols)
    key_rows = local_keys[:, :, :head_cols].reshape(all_questions, -1, heads_here, HD)
    value_rows = local_keys[:, :, head_cols:].reshape(all_questions, -1, heads_here, HD)
    own_counts = lax.dynamic_index_in_dim(counts, group_index, 0, keepdims=False)
    live_slots = own_counts[:, None] > slot_numbers[None, :]
    live_rows = jnp.broadcast_to(live_slots[:, :, None], (all_questions, CAP, passage_len)).reshape(
        all_questions, -1
    )
    scores = jnp.einsum("qthd,qrhd->qhtr", gathered, key_rows, preferred_element_type=jnp.float32)
    scores = jnp.where(live_rows[:, None, None, :], scores, MASKED_SCORE)
    row_peak = over_copies(jnp.max(scores, axis=-1), "qset")
    weights = jnp.where(live_rows[:, None, None, :], jnp.exp(scores - row_peak[..., None]), 0.0)
    group_total = jnp.sum(weights, axis=-1)
    group_summed = jnp.einsum(
        "qhtr,qrhd->qthd",
        weights.astype(jnp.bfloat16),
        value_rows,
        preferred_element_type=jnp.float32,
    )
    summed, row_total = sent_together(
        (group_summed.astype(jnp.bfloat16), group_total.astype(jnp.bfloat16)), "qset", 0, 1
    )
    attended = summed / jnp.transpose(row_total, (0, 2, 1))[..., None]
    attended = attended.astype(jnp.bfloat16).reshape(local_questions * dec_len, head_cols)
    piece_cols = model_width // shard_count
    residual = lax.dynamic_slice_in_dim(dec_states, shard_index * piece_cols, piece_cols, 2).astype(
        jnp.float32
    )
    owned_rows = sent_and_summed(
        lax.dot_general(
            out_weight, attended, (((0,), (1,)), ((), ())), preferred_element_type=jnp.float32
        ).astype(jnp.bfloat16),
        "seq",
        0,
    )
    owned_sum = jnp.transpose(owned_rows).reshape(local_questions, dec_len, piece_cols)
    return (residual + owned_sum).astype(jnp.bfloat16)


def solution(mesh):
    return jax.shard_map(
        body,
        mesh=mesh,
        in_specs=(
            P(("groups", "qset"), "seq", None, None),
            P(),
            P(("groups", "qset"), None, None),
            P(),
            P(None, "seq"),
            P(None, None, "seq"),
            P("seq", None),
            P("groups", None, None),
        ),
        out_specs=P(("groups", "qset"), None, "seq"),
        check_vma=False,
    )
```

profile of v0, /device:TPU:513, one launch (start us, length us, event | category | flops | bytes accessed | tf_op | source)
XLA Modules:
  0.0 255.8 jit_solution(8536282614529816746)
XLA Ops:
  6.5 0.0 copy-start
  6.6 0.0 all-gather.2.cloned.1.call-start
  6.6 0.8 convert_element_type.98
  7.4 0.0 copy-start.4
  7.4 1.6 fusion.8
  9.0 2.6 %fusion.7 = bf16[1,128,4096]{2,1,0:T(8,128)(2,1)} fusion(bf16[1,1,128,4096]{3,2,1,0:T(8,128)(2,1)} %param.8, f32[4096]{0:T(1024)S(1)} %convert_element_type.98, f32[128]{0:T(128)S(1)} %add_rsqrt_fusion.1), kind=kLoop, calls=%fused_computation.16 | loop fusion | flops 2097152 | bytes 2114048 | tf_op jit(solution)/shard_map/convert_element_type | solution.py:80
  11.6 0.1 all-gather.2.cloned.1.call-update
  11.7 0.0 copy-done.4
  11.7 0.0 copy-start.3
  11.7 0.0 copy-done.2
  11.7 0.3 fusion.2
  12.0 0.3 fusion.4
  12.3 0.9 copy-done.3
  13.3 0.4 convolution_convert_fusion.3
  13.7 0.0 copy-start.5
  13.7 0.1 broadcast_in_dim.31
  13.9 1.2 broadcast_bitcast_fusion
  15.1 3.0 %reshape.185 = bf16[8,2,16384]{2,1,0:T(2,128)(2,1)} reshape(bf16[8,2,4,64,64]{4,3,2,1,0:T(8,128)(2,1)} %broadcast_bitcast_fusion) | data formatting | bytes 1048576
  18.1 13.7 %all-to-all-start = ((bf16[8,2,16384]{2,1,0:T(2,128)(2,1)}), bf16[8,2,16384]{2,1,0:T(2,128)(2,1)}, u32[]{:S(2)}, u32[]{:S(2)}) async-start(bf16[8,2,16384]{2,1,0:T(2,128)(2,1)} %reshape.185), calls=%async_computation | async-start | bytes 1048576 | tf_op jit(solution)/shard_map/all_to_all | solution.py:15
  31.8 0.0 copy-done.5
  31.8 0.1 fusion.22
  31.9 4.8 %copy.47 = bf16[512,8,2,256]{3,1,2,0:T(8,128)(2,1)} copy(bf16[512,8,2,256]{3,2,1,0:T(2,128)(2,1)} %bitcast.61) | data formatting | bytes 8388608
  36.8 0.1 convert_reduce_fusion.2
  36.9 0.1 iota_compare_fusion.1
  37.0 0.1 broadcast_in_dim.28
  37.1 0.2 select_reduce_fusion.1
  37.3 6.8 %all-to-all-done = bf16[8,2,16384]{2,1,0:T(2,128)(2,1)} async-done(((bf16[8,2,16384]{2,1,0:T(2,128)(2,1)}), bf16[8,2,16384]{2,1,0:T(2,128)(2,1)}, u32[]{:S(2)}, u32[]{:S(2)}) %all-to-all-start) | async-done | bytes 524320 | tf_op jit(solution)/shard_map/all_to_all | solution.py:15
  44.1 3.1 %reshape.186 = bf16[8,2,4,64,64]{4,3,2,1,0:T(8,128)(2,1)} reshape(bf16[8,2,16384]{2,1,0:T(2,128)(2,1)} %all-to-all-done) | data formatting | bytes 1048576
  47.1 80.0 %all-gather.2.cloned.1.call-done = bf16[16,128,4096]{2,1,0:T(8,128)(2,1)} async-done(((bf16[1,128,4096]{2,1,0:T(8,128)(2,1)}), bf16[16,128,4096]{2,1,0:T(8,128)(2,1)}) %all-gather.2.cloned.1.call-update) | async-done | bytes 16777232 | tf_op jit(solution)/shard_map/all_gather | solution.py:81
  127.2 13.6 %convolution_convert_fusion.1 = bf16[2048,512]{1,0:T(8,128)(2,1)S(1)} fusion(bf16[2048,4096]{1,0:T(8,128)(2,1)} %bitcast.74, bf16[4096,512]{1,0:T(8,128)(2,1)} %bitcast.62), kind=kOutput, calls=%fused_computation.5 | convolution fusion | flops 8590983168 | bytes 23068672 | tf_op jit(solution)/shard_map/dot_general | solution.py:84
  140.8 1.6 convolution_convert_fusion.2
  142.4 2.4 copy.37
  144.8 2.5 fusion.30
  147.3 3.9 %copy.40 = bf16[16,256,256]{1,2,0:T(8,128)(2,1)} copy(bf16[16,256,256]{2,1,0:T(8,128)(2,1)} %get-tuple-element.6) | data formatting | bytes 4194304 | tf_op jit(solution)/shard_map/slice | solution.py:112
  151.2 4.5 %select_reduce_fusion = (f32[16,4,64]{2,1,0:T(4,128)S(1)}, f32[16,4,64,256]{3,2,1,0:T(8,128)}) fusion(pred[16,256]{1,0:T(8,128)(4,1)S(1)} %bitcast.68, bf16[16,64,4,64]{3,1,2,0:T(8,128)(2,1)} %bitcast.59, bf16[16,256,4,64]{1,3,2,0:T(8,128)(2,1)} %bitcast.58), kind=kOutput, calls=%fused_computation.2 | convolution fusion | flops 136310784 | bytes 6836224 | tf_op jit(solution)/shard_map/qthd,qrhd->qhtr/dot_general | solution.py:119
  155.8 0.8 reshape.187
  156.6 6.7 %all-to-all-start.1 = ((f32[8,1,4096]{2,1,0:T(1,128)}), f32[8,1,4096]{2,1,0:T(1,128)S(1)}, u32[]{:S(2)}, u32[]{:S(2)}) async-start(f32[8,1,4096]{2,1,0:T(1,128)} %reshape.187), calls=%async_computation.1 | async-start | bytes 262144 | tf_op jit(solution)/shard_map/all_to_all | solution.py:15
  163.3 3.9 %copy.38 = bf16[16,256,256]{1,2,0:T(8,128)(2,1)} copy(bf16[16,256,256]{2,1,0:T(8,128)(2,1)} %get-tuple-element.5) | data formatting | bytes 4194304 | tf_op jit(solution)/shard_map/slice | solution.py:113
  167.2 4.2 %all-to-all-done.1 = f32[8,1,4096]{2,1,0:T(1,128)S(1)} async-done(((f32[8,1,4096]{2,1,0:T(1,128)}), f32[8,1,4096]{2,1,0:T(1,128)S(1)}, u32[]{:S(2)}, u32[]{:S(2)}) %all-to-all-start.1) | async-done | bytes 131104 | tf_op jit(solution)/shard_map/all_to_all | solution.py:15
  171.5 0.5 broadcast.92
  172.0 1.0 reduce.1
  172.9 0.1 reshape.188
  173.1 0.0 copy-start.1
  173.1 3.3 %fusion = bf16[16,4,64]{2,1,0:T(4,128)(2,1)S(1)} fusion(f32[16,4,64,256]{3,2,1,0:T(8,128)} %get-tuple-element.8, f32[16,4,64]{2,1,0:T(4,128)S(1)} %copy.42, pred[16,256]{1,0:T(8,128)(4,1)S(1)} %bitcast.69), kind=kLoop, calls=%fused_computation.3 | loop fusion | flops 4190208 | bytes 4222976 | tf_op jit(solution)/shard_map/reduce_sum | solution.py:123
  176.4 0.2 copy-done.1
  176.5 3.5 %fusion.19 = bf16[16,64,4,64]{1,3,2,0:T(8,128)(2,1)} fusion(bf16[16,256,4,64]{1,3,2,0:T(8,128)(2,1)} %bitcast.66, f32[16,4,64,256]{3,2,1,0:T(8,128)S(1)} %copy-done.1, f32[16,4,64]{2,1,0:T(4,128)S(1)} %copy.42, pred[16,256]{1,0:T(8,128)(4,1)S(1)} %bitcast.70), kind=kOutput, calls=%fused_computation.26 | convolution fusion | flops 138674176 | bytes 6836224 | tf_op jit(solution)/shard_map/qhtr,qrhd->qthd/dot_general | solution.py:124
  180.0 2.4 copy.43
  182.4 3.3 %concatenate.6 = bf16[8,2,16384]{2,1,0:T(2,128)(2,1)} reshape(bf16[16,64,4,64]{3,2,1,0:T(4,128)(2,1)} %copy.43) | data formatting | bytes 1048576 | tf_op jit(solution)/shard_map/concatenate | solution.py:49
  185.8 0.1 convert_element_type.111
  185.9 1.5 pad_maximum_fusion
  187.4 17.2 %all_to_all.20 = bf16[8,2,16640]{2,1,0:T(2,128)(2,1)S(1)} all-to-all(bf16[8,2,16640]{2,1,0:T(2,128)(2,1)S(1)} %pad_maximum_fusion), channel_id=1, replica_groups=mesh['groups'=2,'seq'=16,'qset'=8] {'qset'}, dimensions={0} | all-to-all | bytes 1064960 | tf_op jit(solution)/shard_map/all_to_all | solution.py:43
  204.6 0.5 convert_reduce_fusion.1
  205.1 0.1 reshape.180
  205.2 0.7 copy.44
  206.0 1.0 div.27
  207.0 0.8 div.28
  207.8 0.1 reshape.179
  208.0 0.0 copy-done
  208.0 1.4 convolution_convert_fusion
  209.3 1.1 copy.53
  210.5 8.4 %all-to-all-start.3 = ((bf16[16,256,128]{1,2,0:T(8,128)(2,1)}), bf16[16,256,128]{1,2,0:T(8,128)(2,1)}, u32[]{:S(2)}, u32[]{:S(2)}) async-start(bf16[16,256,128]{1,2,0:T(8,128)(2,1)} %bitcast.63), calls=%async_computation.3 | async-start | bytes 2097152 | tf_op jit(solution)/shard_map/all_to_all | solution.py:43
  218.8 28.1 %all-to-all-done.3 = bf16[16,256,128]{1,2,0:T(8,128)(2,1)} async-done(((bf16[16,256,128]{1,2,0:T(8,128)(2,1)}), bf16[16,256,128]{1,2,0:T(8,128)(2,1)}, u32[]{:S(2)}, u32[]{:S(2)}) %all-to-all-start.3) | async-done | bytes 1048608 | tf_op jit(solution)/shard_map/all_to_all | solution.py:43
  246.9 1.4 convert_reduce_fusion
  248.3 0.7 add_convert_fusion
  (16 shorter events, 0.2 us)
Async XLA Ops:
  6.5 201.4 %copy-start = (bf16[256,4096]{1,0:T(8,128)(2,1)S(1)}, bf16[256,4096]{1,0:T(8,128)(2,1)}, u32[]{:S(2)}) copy-start(bf16[256,4096]{1,0:T(8,128)(2,1)} %param.14) | copy-start | bytes 6291460
  6.6 120.6 %all-gather.2.cloned.1.call-start = ((), (), s32[]{:S(2)}) async-start(), calls=%async_computation.4 | async-start | bytes 17825792 | tf_op jit(solution)/shard_map/all_gather | solution.py:81
  7.4 4.3 %copy-start.4 = (bf16[4096]{0:T(1024)(128)(2,1)S(1)}, bf16[4096]{0:T(1024)(128)(2,1)}, u32[]{:S(2)}) copy-start(bf16[4096]{0:T(1024)(128)(2,1)} %param.11) | copy-start | bytes 24580
  7.4 4.3 %copy-start.2 = (bf16[2,64,4096]{2,1,0:T(8,128)(2,1)S(1)}, bf16[2,64,4096]{2,1,0:T(8,128)(2,1)}, u32[]{:S(2)}) copy-start(bf16[2,64,4096]{2,1,0:T(8,128)(2,1)} %param.10) | copy-start | bytes 3145732
  11.7 1.6 copy-start.3
  13.7 18.1 %copy-start.5 = (s32[8,16,1]{1,2,0:T(1,128)S(1)}, s32[8,16,1]{1,2,0:T(1,128)}, u32[]{:S(2)}) copy-start(s32[8,16,1]{1,2,0:T(1,128)} %param.15) | copy-start | bytes 1540
  18.1 25.9 %all-to-all-start = ((bf16[8,2,16384]{2,1,0:T(2,128)(2,1)}), bf16[8,2,16384]{2,1,0:T(2,128)(2,1)}, u32[]{:S(2)}, u32[]{:S(2)}) async-start(bf16[8,2,16384]{2,1,0:T(2,128)(2,1)} %reshape.185), calls=%async_computation | async-start | bytes 1048576 | tf_op jit(solution)/shard_map/all_to_all | solution.py:15
  156.6 14.9 %all-to-all-start.1 = ((f32[8,1,4096]{2,1,0:T(1,128)}), f32[8,1,4096]{2,1,0:T(1,128)S(1)}, u32[]{:S(2)}, u32[]{:S(2)}) async-start(f32[8,1,4096]{2,1,0:T(1,128)} %reshape.187), calls=%async_computation.1 | async-start | bytes 262144 | tf_op jit(solution)/shard_map/all_to_all | solution.py:15
  173.1 3.5 %copy-start.1 = (f32[16,4,64,256]{3,2,1,0:T(8,128)S(1)}, f32[16,4,64,256]{3,2,1,0:T(8,128)}, u32[]{:S(2)}) copy-start(f32[16,4,64,256]{3,2,1,0:T(8,128)} %get-tuple-element.8) | copy-start | bytes 12582916
  210.5 36.5 %all-to-all-start.3 = ((bf16[16,256,128]{1,2,0:T(8,128)(2,1)}), bf16[16,256,128]{1,2,0:T(8,128)(2,1)}, u32[]{:S(2)}, u32[]{:S(2)}) async-start(bf16[16,256,128]{1,2,0:T(8,128)(2,1)} %bitcast.63), calls=%async_computation.3 | async-start | bytes 2097152 | tf_op jit(solution)/shard_map/all_to_all | solution.py:43
Sparse Core Ops, SparseCore 0:
  11.8 115.3 all-gather.1
where the time goes:
time: 257 us; the launch traced here: 256 us
  waiting for transfers between devices  119 us (46%)
  local copies, waits for them, and re-layouts  37.5 us (15%)
  starting transfers between devices  28.8 us (11%)
  matrix products  25 us (10%)
  blocking collectives  17.2 us (7%)
  other arithmetic  14.4 us (6%)
  between operations  13.7 us (5%)
    all_gather x1, waiting for transfers between devices, body(): gathered_rows = lax.all_gather(own_rows, 'seq', axis=0, tiled=True)  80 us
    all_to_all x1, waiting for transfers between devices, sent_and_summed(): lax.all_to_all(pieces, axis, split_axis=0, concat_axis=0, tiled=True)  28.1 us
    all_to_all x2, starting transfers between devices, from_everyone(): lax.all_to_all(jnp.broadcast_to(shard[None], (devices, *shard.shape)), ax...  20.4 us
    all_to_all x1, blocking collectives, sent_and_summed(): lax.all_to_all(pieces, axis, split_axis=0, concat_axis=0, tiled=True)  17.2 us
    unnamed x20, local copies, waits for them, and re-layouts  14.2 us
    dot_general x1, matrix products, body(): product = jnp.dot(flat_rows, kv_weight, preferred_element_type=jnp.float32)  13.6 us
    all_to_all x2, waiting for transfers between devices, from_everyone(): lax.all_to_all(jnp.broadcast_to(shard[None], (devices, *shard.shape)), ax...  11 us
    all_to_all x1, starting transfers between devices, sent_and_summed(): lax.all_to_all(pieces, axis, split_axis=0, concat_axis=0, tiled=True)  8.36 us
  transfers between devices with their start and end apart: 4, of which 4 were waited for; matrix products, arithmetic and copies ran while one was open for 7% of the time, Pallas kernels for 0%

commit v1 on v0

--- a/solution.py
+++ b/solution.py
@@ -78,7 +78,10 @@
     all_questions = local_questions * group_count
     kv_weight = key_value_weight.reshape(model_width, 2 * head_cols)
     own_rows = scaled_norm(states[0, 0], enc_gain).astype(jnp.bfloat16)[None]
-    gathered_rows = lax.all_gather(own_rows, "seq", axis=0, tiled=True)
+    devices_2 = lax.axis_size("seq")
+    shards = jnp.stack([own_rows for _ in range(devices_2)])
+    shards = lax.all_to_all(shards, "seq", split_axis=0, concat_axis=0)
+    gathered_rows = jnp.concatenate(shards, axis=0)
     piece_count = gathered_rows.shape[0]
     flat_rows = gathered_rows.reshape(piece_count * passage_len, model_width)
     product = jnp.dot(flat_rows, kv_weight, preferred_element_type=jnp.float32)

time: 257 us -> 535 us (2.08)
  waiting for transfers between devices: 119 us -> 397 us
  starting transfers between devices: 28.8 us -> 44.2 us
  between operations: 13.7 us -> 0.28 us
    all_to_all x0 -> x1, waiting for transfers between devices: none -> 356 us  [body(): shards = lax.all_to_all(shards, 'seq', split_axis=0, concat_axis=0)]
    all_gather x1 -> x0, waiting for transfers between devices: 80 us -> none  [body(): gathered_rows = lax.all_gather(own_rows, 'seq', axis=0, tiled=True)]
    all_to_all x0 -> x1, starting transfers between devices: none -> 17 us  [body(): shards = lax.all_to_all(shards, 'seq', split_axis=0, concat_axis=0)]
    another operation x0 -> x1, local copies, waits for them, and re-layouts: none -> 5.92 us  [body(): shards = jnp.stack([own_rows for _ in range(devices_2)])]
  transfers between devices with their start and end apart: 4 -> 4, of which waited for: 4 -> 4; matrix products, arithmetic and copies ran while one was open for 7% -> 3% of each run, Pallas kernels for 0% -> 0%
where the time goes in v1:
time: 535 us; the launch traced here: 534 us
  waiting for transfers between devices  397 us (74%)
  starting transfers between devices  44.2 us (8%)
  local copies, waits for them, and re-layouts  37.2 us (7%)
  matrix products  23.8 us (4%)
  blocking collectives  17.4 us (3%)
  other arithmetic  14.2 us (3%)
    all_to_all x1, waiting for transfers between devices, body(): shards = lax.all_to_all(shards, 'seq', split_axis=0, concat_axis=0)  356 us
    all_to_all x1, waiting for transfers between devices, sent_and_summed(): lax.all_to_all(pieces, axis, split_axis=0, concat_axis=0, tiled=True)  28 us
    all_to_all x2, starting transfers between devices, from_everyone(): lax.all_to_all(jnp.broadcast_to(shard[None], (devices, *shard.shape)), ax...  17.5 us
    all_to_all x1, blocking collectives, sent_and_summed(): lax.all_to_all(pieces, axis, split_axis=0, concat_axis=0, tiled=True)  17.4 us
    all_to_all x1, starting transfers between devices, body(): shards = lax.all_to_all(shards, 'seq', split_axis=0, concat_axis=0)  17 us
    all_to_all x2, waiting for transfers between devices, from_everyone(): lax.all_to_all(jnp.broadcast_to(shard[None], (devices, *shard.shape)), ax...  13.7 us
    dot_general x1, matrix products, body(): product = jnp.dot(flat_rows, kv_weight, preferred_element_type=jnp.float32)  13.6 us
    unnamed x20, local copies, waits for them, and re-layouts  12.7 us
  transfers between devices with their start and end apart: 4, of which 4 were waited for; matrix products, arithmetic and copies ran while one was open for 3% of the time, Pallas kernels for 0%

profile of v1, /device:TPU:513, one launch (start us, length us, event | category | flops | bytes accessed | tf_op | source)
XLA Modules:
  0.0 534.4 jit_solution(2680741458143424060)
XLA Ops:
  0.0 0.0 copy-start
  0.0 0.0 copy-start.3
  0.0 0.9 convert_element_type.85
  0.9 1.6 fusion.5
  2.5 1.6 fusion.7
  4.1 0.0 copy-done.3
  4.1 0.4 convolution_convert_fusion.3
  4.5 0.0 copy-start.4
  4.5 0.0 copy-start.2
  4.5 0.1 broadcast_in_dim.31
  4.7 1.2 broadcast_bitcast_fusion
  5.9 3.0 reshape.135
  9.0 13.7 %all-to-all-start.1 = ((bf16[8,2,16384]{2,1,0:T(2,128)(2,1)}), bf16[8,2,16384]{2,1,0:T(2,128)(2,1)}, u32[]{:S(2)}, u32[]{:S(2)}) async-start(bf16[8,2,16384]{2,1,0:T(2,128)(2,1)} %reshape.135), calls=%async_computation.1 | async-start | bytes 1048576 | tf_op jit(solution)/shard_map/all_to_all | solution.py:15
  22.7 0.0 copy-done.4
  22.7 0.0 copy-done.2
  22.7 0.3 fusion.2
  23.0 1.6 fusion.21
  24.5 10.4 %all-to-all-done.1 = bf16[8,2,16384]{2,1,0:T(2,128)(2,1)} async-done(((bf16[8,2,16384]{2,1,0:T(2,128)(2,1)}), bf16[8,2,16384]{2,1,0:T(2,128)(2,1)}, u32[]{:S(2)}, u32[]{:S(2)}) %all-to-all-start.1) | async-done | bytes 524320 | tf_op jit(solution)/shard_map/all_to_all | solution.py:15
  34.9 5.9 %stack.3 = bf16[16,1,128,4096]{3,2,1,0:T(8,128)(2,1)} broadcast(bf16[128,4096]{1,0:T(8,128)(2,1)S(1)} %fusion.21), dimensions={2,3} | broadcast | bytes 17825792 | tf_op jit(solution)/shard_map/stack | solution.py:82
  40.8 17.0 %all-to-all-start = ((bf16[16,1,128,4096]{3,2,1,0:T(8,128)(2,1)}), bf16[16,1,128,4096]{3,2,1,0:T(8,128)(2,1)}, u32[]{:S(2)}, u32[]{:S(2)}) async-start(bf16[16,1,128,4096]{3,2,1,0:T(8,128)(2,1)} %stack.3), calls=%async_computation | async-start | bytes 33554432 | tf_op jit(solution)/shard_map/all_to_all | solution.py:83
  57.8 0.0 copy-done.5
  57.8 0.1 fusion.22
  57.9 5.0 copy.47
  62.9 0.1 convert_reduce_fusion.2
  63.0 0.1 iota_compare_fusion.1
  63.1 0.1 broadcast_in_dim.28
  63.2 0.2 select_reduce_fusion.1
  63.4 2.3 reshape.136
  65.7 355.6 %all-to-all-done = bf16[16,1,128,4096]{3,2,1,0:T(8,128)(2,1)} async-done(((bf16[16,1,128,4096]{3,2,1,0:T(8,128)(2,1)}), bf16[16,1,128,4096]{3,2,1,0:T(8,128)(2,1)}, u32[]{:S(2)}, u32[]{:S(2)}) %all-to-all-start) | async-done | bytes 16777248 | tf_op jit(solution)/shard_map/all_to_all | solution.py:83
  421.3 13.6 %convolution_convert_fusion.1 = bf16[2048,512]{1,0:T(8,128)(2,1)S(1)} fusion(bf16[2048,4096]{1,0:T(8,128)(2,1)} %bitcast.3, bf16[4096,512]{1,0:T(8,128)(2,1)} %bitcast.56), kind=kOutput, calls=%fused_computation.5 | convolution fusion | flops 8590983168 | bytes 23068672 | tf_op jit(solution)/shard_map/dot_general | solution.py:87
  434.8 1.6 convolution_convert_fusion.2
  436.4 2.4 copy.37
  438.8 2.5 fusion.30
  441.3 3.9 copy.40
  445.2 4.2 select_reduce_fusion
  449.5 0.8 reshape.137
  450.3 3.8 all-to-all-start.2
  454.1 3.9 copy.38
  458.1 3.4 all-to-all-done.2
  461.4 0.5 broadcast.64
  461.9 1.0 reduce.1
  462.9 0.1 reshape.138
  463.1 0.0 copy-start.1
  463.1 3.3 fusion
  466.4 0.2 copy-done.1
  466.5 3.5 fusion.18
  470.0 1.7 copy.43
  471.7 1.5 concatenate.6
  473.2 0.1 convert_element_type.92
  473.3 1.5 pad_maximum_fusion
  474.8 17.4 %all_to_all.25 = bf16[8,2,16640]{2,1,0:T(2,128)(2,1)S(1)} all-to-all(bf16[8,2,16640]{2,1,0:T(2,128)(2,1)S(1)} %pad_maximum_fusion), channel_id=1, replica_groups=mesh['groups'=2,'seq'=16,'qset'=8] {'qset'}, dimensions={0} | all-to-all | bytes 1064960 | tf_op jit(solution)/shard_map/all_to_all | solution.py:43
  492.2 0.5 convert_reduce_fusion.1
  492.7 0.1 reshape.131
  492.8 0.1 copy.44
  492.9 0.2 div.27
  493.1 0.2 div.28
  493.3 0.1 reshape.130
  493.4 0.0 copy-done
  493.4 0.4 convolution_convert_fusion
  493.9 1.1 copy.53
  495.0 9.8 %all-to-all-start.4 = ((bf16[16,256,128]{1,2,0:T(8,128)(2,1)}), bf16[16,256,128]{1,2,0:T(8,128)(2,1)S(1)}, u32[]{:S(2)}, u32[]{:S(2)}) async-start(bf16[16,256,128]{1,2,0:T(8,128)(2,1)} %bitcast.57), calls=%async_computation.4 | async-start | bytes 2097152 | tf_op jit(solution)/shard_map/all_to_all | solution.py:43
  504.8 28.0 %all-to-all-done.4 = bf16[16,256,128]{1,2,0:T(8,128)(2,1)S(1)} async-done(((bf16[16,256,128]{1,2,0:T(8,128)(2,1)}), bf16[16,256,128]{1,2,0:T(8,128)(2,1)S(1)}, u32[]{:S(2)}, u32[]{:S(2)}) %all-to-all-start.4) | async-done | bytes 1048608 | tf_op jit(solution)/shard_map/all_to_all | solution.py:43
  532.7 0.1 convert_reduce_fusion
  532.9 1.5 add_convert_fusion
  (16 shorter events, 0.2 us)
Async XLA Ops:
  0.0 493.4 %copy-start = (bf16[256,4096]{1,0:T(8,128)(2,1)S(1)}, bf16[256,4096]{1,0:T(8,128)(2,1)}, u32[]{:S(2)}) copy-start(bf16[256,4096]{1,0:T(8,128)(2,1)} %param.14) | copy-start | bytes 6291460
  0.0 4.1 copy-start.3
  4.5 18.1 %copy-start.4 = (bf16[4096]{0:T(1024)(128)(2,1)S(1)}, bf16[4096]{0:T(1024)(128)(2,1)}, u32[]{:S(2)}) copy-start(bf16[4096]{0:T(1024)(128)(2,1)} %param.9) | copy-start | bytes 24580
  4.5 18.1 %copy-start.2 = (bf16[1,1,128,4096]{3,2,1,0:T(8,128)(2,1)S(1)}, bf16[1,1,128,4096]{3,2,1,0:T(8,128)(2,1)}, u32[]{:S(2)}) copy-start(bf16[1,1,128,4096]{3,2,1,0:T(8,128)(2,1)} %param.8) | copy-start | bytes 3145732
  9.0 25.9 %all-to-all-start.1 = ((bf16[8,2,16384]{2,1,0:T(2,128)(2,1)}), bf16[8,2,16384]{2,1,0:T(2,128)(2,1)}, u32[]{:S(2)}, u32[]{:S(2)}) async-start(bf16[8,2,16384]{2,1,0:T(2,128)(2,1)} %reshape.135), calls=%async_computation.1 | async-start | bytes 1048576 | tf_op jit(solution)/shard_map/all_to_all | solution.py:15
  40.8 17.0 %copy-start.5 = (s32[8,16,1]{1,2,0:T(1,128)S(1)}, s32[8,16,1]{1,2,0:T(1,128)}, u32[]{:S(2)}) copy-start(s32[8,16,1]{1,2,0:T(1,128)} %param.15) | copy-start | bytes 1540
  40.8 380.4 %all-to-all-start = ((bf16[16,1,128,4096]{3,2,1,0:T(8,128)(2,1)}), bf16[16,1,128,4096]{3,2,1,0:T(8,128)(2,1)}, u32[]{:S(2)}, u32[]{:S(2)}) async-start(bf16[16,1,128,4096]{3,2,1,0:T(8,128)(2,1)} %stack.3), calls=%async_computation | async-start | bytes 33554432 | tf_op jit(solution)/shard_map/all_to_all | solution.py:83
  450.3 11.1 %all-to-all-start.2 = ((f32[8,1,4096]{2,1,0:T(1,128)}), f32[8,1,4096]{2,1,0:T(1,128)S(1)}, u32[]{:S(2)}, u32[]{:S(2)}) async-start(f32[8,1,4096]{2,1,0:T(1,128)} %reshape.137), calls=%async_computation.2 | async-start | bytes 262144 | tf_op jit(solution)/shard_map/all_to_all | solution.py:15
  463.1 3.5 copy-start.1
  495.0 37.7 %all-to-all-start.4 = ((bf16[16,256,128]{1,2,0:T(8,128)(2,1)}), bf16[16,256,128]{1,2,0:T(8,128)(2,1)S(1)}, u32[]{:S(2)}, u32[]{:S(2)}) async-start(bf16[16,256,128]{1,2,0:T(8,128)(2,1)} %bitcast.57), calls=%async_computation.4 | async-start | bytes 2097152 | tf_op jit(solution)/shard_map/all_to_all | solution.py:43
